TPU v7x, 32 devices: a whole 2x2x4 slice. The times are simulated.
32 devices in a mesh: groups: 2 (over x), replica: 16 (over z, y, core).
Axes of the slice: x: 2, y: 2, z: 4, core: 2. Of those that a mesh axis runs over, the one named last changes fastest.
Arguments:
- tokens: bfloat16 [32768, 2048], P(('groups', 'replica')), parts along dimension 0, may hold values from -6 to 6
- pseudo_keys: bfloat16 [32, 2048, 512], P(('groups', 'replica')), parts along dimension 0, may hold values from -0.875 to 0.875
- pseudo_values: bfloat16 [32, 2048, 512], P(('groups', 'replica')), parts along dimension 0, may hold values from -0.875 to 0.875
- master_keys: float32 [4096, 512], P(('groups', 'replica')), parts along dimension 0, may hold values from -0.125 to 0.125
- moment_keys: float32 [4096, 512], P(('groups', 'replica')), parts along dimension 0, may hold values from -0.125 to 0.125
- master_values: float32 [4096, 512], P(('groups', 'replica')), parts along dimension 0, may hold values from -0.125 to 0.125
- moment_values: float32 [4096, 512], P(('groups', 'replica')), parts along dimension 0, may hold values from -0.125 to 0.125
- outer_hyper: float32 [4], P('groups'), parts along dimension 0, may hold values from 0.5 to 0.95
Outputs:
- eval_keys: bfloat16 [32768, 512], P(('groups', 'replica')), parts along dimension 0
- eval_values: bfloat16 [32768, 512], P(('groups', 'replica')), parts along dimension 0
- new_master_keys: float32 [4096, 512], P(('groups', 'replica')), parts along dimension 0
- new_moment_keys: float32 [4096, 512], P(('groups', 'replica')), parts along dimension 0
- new_master_values: float32 [4096, 512], P(('groups', 'replica')), parts along dimension 0
- new_moment_values: float32 [4096, 512], P(('groups', 'replica')), parts along dimension 0
There are 2 independent parts, one for each index of `groups`. A program takes and returns all parts, laid end to end along the dimension named above; each array names one. Nothing has to cross between parts.
All inputs are finite; a program needn't handle non-finite values.
Results may differ from a plain program's by a relative error of at most 0.0049.
Values may be sent and summed in bfloat16 or wider, within the bound.
A program may use at most 128 MiB of HBM per device.

v0:
```python
import jax
import jax.numpy as jnp
from jax import lax
from jax.sharding import PartitionSpec as P


def body(
    tokens,
    pseudo_keys,
    pseudo_values,
    master_keys,
    moment_keys,
    master_values,
    moment_values,
    outer_hyper,
):
    outer_rate = outer_hyper[0]
    outer_mom = outer_hyper[1]
    replicas = lax.axis_size("replica")
    width = master_keys.shape[1]

    def nesterov(summed, master, moment):
        averaged = summed / replicas
        moment_new = outer_mom * moment + averaged
        master_new = master - outer_rate * (averaged + outer_mom * moment_new)
        return (master_new, moment_new)

    blocks_keys = pseudo_keys[0].reshape(replicas, -1, width)
    blocks_values = pseudo_values[0].reshape(replicas, -1, width)
    owned_keys, owned_values = (
        lax.all_to_all(blocks_keys, "replica", split_axis=0, concat_axis=0, tiled=True),
        lax.all_to_all(blocks_values, "replica", split_axis=0, concat_axis=0, tiled=True),
    )
    summed_keys = jnp.sum(owned_keys.astype(jnp.float32), axis=0)
    summed_values = jnp.sum(owned_values.astype(jnp.float32), axis=0)
    master_k, moment_k = nesterov(summed_keys, master_keys, moment_keys)
    master_v, moment_v = nesterov(summed_values, master_values, moment_values)
    whole_keys, whole_values = (
        lax.all_gather(master_k.astype(jnp.bfloat16), "replica", axis=0, tiled=True),
        lax.all_gather(master_v.astype(jnp.bfloat16), "replica", axis=0, tiled=True),
    )
    projected_keys = jnp.dot(tokens, whole_keys, preferred_element_type=jnp.float32)
    projected_values = jnp.dot(tokens, whole_values, preferred_element_type=jnp.float32)
    return (
        projected_keys.astype(jnp.bfloat16),
        projected_values.astype(jnp.bfloat16),
        master_k,
        moment_k,
        master_v,
        moment_v,
    )


def solution(mesh):
    in_specs = (
        P(("groups", "replica"), None),
        P(("groups", "replica"), None, None),
        P(("groups", "replica"), None, None),
        P(("groups", "replica"), None),
        P(("groups", "replica"), None),
        P(("groups", "replica"), None),
        P(("groups", "replica"), None),
        P("groups"),
    )
    out_specs = (
        P(("groups", "replica"), None),
        P(("groups", "replica"), None),
        P(("groups", "replica"), None),
        P(("groups", "replica"), None),
        P(("groups", "replica"), None),
        P(("groups", "replica"), None),
    )
    return jax.shard_map(body, mesh=mesh, in_specs=in_specs, out_specs=out_specs, check_vma=False)
```

profile of v0, /device:TPU:0, one launch (start us, length us, event | category | flops | bytes accessed | tf_op | source)
XLA Modules:
  0.0 186.3 jit_solution(580788009205399574)
XLA Ops:
  7.2 7.4 %all-to-all-start.1 = ((bf16[16,128,512]{2,1,0:T(8,128)(2,1)}), bf16[16,128,512]{2,1,0:T(8,128)(2,1)S(1)}, u32[]{:S(2)}, u32[]{:S(2)}) async-start(bf16[16,128,512]{2,1,0:T(8,128)(2,1)} %bitcast.12), calls=%async_computation.1 | async-start | bytes 4194304 | tf_op jit(solution)/shard_map/all_to_all | solution.py:32
  14.6 0.6 fusion.4
  15.2 40.4 %all-to-all-done.1 = bf16[16,128,512]{2,1,0:T(8,128)(2,1)S(1)} async-done(((bf16[16,128,512]{2,1,0:T(8,128)(2,1)}), bf16[16,128,512]{2,1,0:T(8,128)(2,1)S(1)}, u32[]{:S(2)}, u32[]{:S(2)}) %all-to-all-start.1) | async-done | bytes 2097184 | tf_op jit(solution)/shard_map/all_to_all | solution.py:32
  55.6 1.3 copy-done
  56.9 11.2 %all-to-all-start = ((bf16[16,128,512]{2,1,0:T(8,128)(2,1)}), bf16[16,128,512]{2,1,0:T(8,128)(2,1)S(1)}, u32[]{:S(2)}, u32[]{:S(2)}) async-start(bf16[16,128,512]{2,1,0:T(8,128)(2,1)} %bitcast.13), calls=%async_computation | async-start | bytes 4194304 | tf_op jit(solution)/shard_map/all_to_all | solution.py:31
  68.1 0.0 copy-start.1
  68.1 0.0 copy-start.2
  68.2 0.0 all-gather.5.cloned.1.call-start
  68.2 2.0 %convert_reduce_fusion = f32[128,512]{1,0:T(8,128)S(1)} fusion(bf16[16,128,512]{2,1,0:T(8,128)(2,1)} %copy-done), kind=kLoop, calls=%fused_computation | loop fusion | flops 2031616 | bytes 2359296 | tf_op jit(solution)/shard_map/reduce_sum | solution.py:35
  70.2 0.0 copy-start.3
  70.2 0.0 copy-start.4
  70.2 2.2 %fusion.2 = (bf16[128,512]{1,0:T(8,128)(2,1)}, f32[128,512]{1,0:T(8,128)}, f32[128,512]{1,0:T(8,128)}) fusion(f32[128,512]{1,0:T(8,128)S(1)} %copy-done.1, f32[]{:T(128)} %bitcast.2, f32[128,512]{1,0:T(8,128)S(1)} %convert_reduce_fusion, f32[]{:T(128)} %bitcast, f32[128,512]{1,0:T(8,128)S(1)} %copy-done.2), kind=kLoop, calls=%fused_computation.10 | loop fusion | flops 524288 | bytes 1441800 | tf_op jit(solution)/shard_map/convert_element_type | solution.py:40
  72.4 0.0 all-gather.5.cloned.1.call-update
  72.4 0.0 all-gather.3.cloned.1.call-start
  72.5 40.8 %all-to-all-done = bf16[16,128,512]{2,1,0:T(8,128)(2,1)S(1)} async-done(((bf16[16,128,512]{2,1,0:T(8,128)(2,1)}), bf16[16,128,512]{2,1,0:T(8,128)(2,1)S(1)}, u32[]{:S(2)}, u32[]{:S(2)}) %all-to-all-start) | async-done | bytes 2097184 | tf_op jit(solution)/shard_map/all_to_all | solution.py:31
  113.3 0.3 convert_reduce_fusion.1
  113.6 2.1 %fusion.3 = (bf16[128,512]{1,0:T(8,128)(2,1)}, f32[128,512]{1,0:T(8,128)}, f32[128,512]{1,0:T(8,128)}) fusion(f32[128,512]{1,0:T(8,128)S(1)} %copy-done.3, f32[]{:T(128)} %bitcast.2, f32[128,512]{1,0:T(8,128)S(1)} %convert_reduce_fusion.1, f32[]{:T(128)} %bitcast, f32[128,512]{1,0:T(8,128)S(1)} %copy-done.4), kind=kLoop, calls=%fused_computation.11 | loop fusion | flops 524288 | bytes 1441800 | tf_op jit(solution)/shard_map/convert_element_type | solution.py:39
  115.8 0.0 all-gather.3.cloned.1.call-update
  115.8 13.9 %all-gather.5.cloned.1.call-done = bf16[2048,512]{1,0:T(8,128)(2,1)} async-done(((bf16[128,512]{1,0:T(8,128)(2,1)}), bf16[2048,512]{1,0:T(8,128)(2,1)}) %all-gather.5.cloned.1.call-update) | async-done | bytes 2097168 | tf_op jit(solution)/shard_map/all_gather | solution.py:40
  129.7 5.2 %fusion.1 = bf16[1024,512]{0,1:T(8,128)(2,1)S(1)} fusion(bf16[2048,512]{1,0:T(8,128)(2,1)} %all-gather.5.cloned.1.call-done, bf16[1024,2048]{1,0:T(8,128)(2,1)} %param.8), kind=kOutput, calls=%fused_computation.5 | convolution fusion | flops 2148007936 | bytes 7340032 | tf_op jit(solution)/shard_map/dot_general | solution.py:43
  134.9 1.3 copy.15
  136.2 36.7 %all-gather.3.cloned.1.call-done = bf16[2048,512]{1,0:T(8,128)(2,1)} async-done(((bf16[128,512]{1,0:T(8,128)(2,1)}), bf16[2048,512]{1,0:T(8,128)(2,1)}) %all-gather.3.cloned.1.call-update) | async-done | bytes 2097168 | tf_op jit(solution)/shard_map/all_gather | solution.py:39
  172.9 5.2 %fusion = bf16[1024,512]{0,1:T(8,128)(2,1)S(1)} fusion(bf16[2048,512]{1,0:T(8,128)(2,1)} %all-gather.3.cloned.1.call-done, bf16[1024,2048]{1,0:T(8,128)(2,1)} %param.8), kind=kOutput, calls=%fused_computation.4 | convolution fusion | flops 2148007936 | bytes 7340032 | tf_op jit(solution)/shard_map/dot_general | solution.py:42
  178.1 1.3 copy.14
  (7 shorter events, 0.0 us)
Async XLA Ops:
  7.2 7.4 %copy-start.5 = (f32[2]{0:T(128)S(1)}, f32[2]{0:T(128)}, u32[]{:S(2)}) copy-start(f32[2]{0:T(128)} %param.15) | copy-start | bytes 28
  7.2 48.4 %all-to-all-start.1 = ((bf16[16,128,512]{2,1,0:T(8,128)(2,1)}), bf16[16,128,512]{2,1,0:T(8,128)(2,1)S(1)}, u32[]{:S(2)}, u32[]{:S(2)}) async-start(bf16[16,128,512]{2,1,0:T(8,128)(2,1)} %bitcast.12), calls=%async_computation.1 | async-start | bytes 4194304 | tf_op jit(solution)/shard_map/all_to_all | solution.py:32
  55.6 1.3 copy-start
  56.9 56.4 %all-to-all-start = ((bf16[16,128,512]{2,1,0:T(8,128)(2,1)}), bf16[16,128,512]{2,1,0:T(8,128)(2,1)S(1)}, u32[]{:S(2)}, u32[]{:S(2)}) async-start(bf16[16,128,512]{2,1,0:T(8,128)(2,1)} %bitcast.13), calls=%async_computation | async-start | bytes 4194304 | tf_op jit(solution)/shard_map/all_to_all | solution.py:31
  68.1 2.1 %copy-start.1 = (f32[128,512]{1,0:T(8,128)S(1)}, f32[128,512]{1,0:T(8,128)}, u32[]{:S(2)}) copy-start(f32[128,512]{1,0:T(8,128)} %param.13) | copy-start | bytes 786436
  68.1 2.1 %copy-start.2 = (f32[128,512]{1,0:T(8,128)S(1)}, f32[128,512]{1,0:T(8,128)}, u32[]{:S(2)}) copy-start(f32[128,512]{1,0:T(8,128)} %param.14) | copy-start | bytes 786436
  68.2 61.5 %all-gather.5.cloned.1.call-start = ((), (), s32[]{:S(2)}) async-start(), calls=%async_computation.3 | async-start | bytes 2228224 | tf_op jit(solution)/shard_map/all_gather | solution.py:40
  70.2 43.5 %copy-start.3 = (f32[128,512]{1,0:T(8,128)S(1)}, f32[128,512]{1,0:T(8,128)}, u32[]{:S(2)}) copy-start(f32[128,512]{1,0:T(8,128)} %param.11) | copy-start | bytes 786436
  70.2 43.5 %copy-start.4 = (f32[128,512]{1,0:T(8,128)S(1)}, f32[128,512]{1,0:T(8,128)}, u32[]{:S(2)}) copy-start(f32[128,512]{1,0:T(8,128)} %param.12) | copy-start | bytes 786436
  72.4 100.5 %all-gather.3.cloned.1.call-start = ((), (), s32[]{:S(2)}) async-start(), calls=%async_computation.2 | async-start | bytes 2228224 | tf_op jit(solution)/shard_map/all_gather | solution.py:39
Sparse Core Ops, SparseCore 0:
  72.6 57.1 all-gather.4
  132.4 40.4 all-gather.2
where the time goes:
time: 187 us; the launch traced here: 186 us
  waiting for transfers between devices  132 us (71%)
  starting transfers between devices  18.7 us (10%)
  between operations  14.2 us (8%)
  matrix products  10.4 us (6%)
  other arithmetic  6.59 us (4%)
  local copies, waits for them, and re-layouts  4.62 us (2%)
    all_to_all x1, waiting for transfers between devices, body(): lax.all_to_all(blocks_keys, 'replica', split_axis=0, concat_axis=0, tiled...  40.8 us
    all_to_all x1, waiting for transfers between devices, body(): lax.all_to_all(blocks_values, 'replica', split_axis=0, concat_axis=0, til...  40.4 us
    all_gather x1, waiting for transfers between devices, body(): lax.all_gather(master_k.astype(jnp.bfloat16), 'replica', axis=0, tiled=True)  36.7 us
    all_gather x1, waiting for transfers between devices, body(): lax.all_gather(master_v.astype(jnp.bfloat16), 'replica', axis=0, tiled=True)  13.9 us
    all_to_all x1, starting transfers between devices, body(): lax.all_to_all(blocks_keys, 'replica', split_axis=0, concat_axis=0, tiled...  11.2 us
    all_to_all x1, starting transfers between devices, body(): lax.all_to_all(blocks_values, 'replica', split_axis=0, concat_axis=0, til...  7.43 us
    dot_general x1, matrix products, body(): jnp.dot(tokens, whole_values, preferred_element_type=jnp.float32)  5.2 us
    dot_general x1, matrix products, body(): jnp.dot(tokens, whole_keys, preferred_element_type=jnp.float32)  5.2 us
  transfers between devices with their start and end apart: 4, of which 4 were waited for; matrix products, arithmetic and copies ran while one was open for 7% of the time, Pallas kernels for 0%

commit v1 on v0

v1 whole, which is shorter than its diff:
```python
import functools

import jax
import jax.numpy as jnp
from jax import lax
from jax.experimental import pallas as pl
from jax.experimental.pallas import tpu as pltpu
from jax.sharding import PartitionSpec as P

MESH = pl.DeviceIdType.MESH
F32 = jnp.float32
BF16 = jnp.bfloat16


def kernel(
    Z,
    Y,
    replicas,
    tokens,
    pseudo_keys,
    pseudo_values,
    master_keys,
    moment_keys,
    master_values,
    moment_values,
    hyper,
    eval_keys,
    eval_values,
    out_master_keys,
    out_moment_keys,
    out_master_values,
    out_moment_values,
    tok,
    mine,
    from_core,
    to_y,
    from_y,
    to_z,
    from_left,
    from_right,
    weights,
    total,
    acc,
    result,
    master,
    moment,
    load_sem,
    state_sem,
    tok_sem,
    store_sem,
    rc_s,
    rc_r,
    ry_s,
    ry_r,
    rz_s,
    rl_r,
    rr_r,
    gr_s,
    gl_s,
    gz_r,
    gy_s,
    gy_r,
    gc_s,
    gc_r,
):
    me = lax.axis_index("replica")
    core = lax.rem(me, 2)
    chip = lax.div(me, 2)
    y = lax.rem(chip, Y)
    z = lax.div(chip, Y)
    oc = 1 - core
    oy = 1 - y

    def dev(zz, yy, cc):
        return {"replica": (zz * Y + yy) * 2 + cc}

    pseudo = (pseudo_keys, pseudo_values)
    rows = mine.shape[3]

    loads = [
        pltpu.make_async_copy(pseudo[kv].at[:, :, core], mine.at[kv], load_sem.at[kv])
        for kv in range(2)
    ]
    states = [
        pltpu.make_async_copy(src, dst, state_sem.at[i])
        for i, (src, dst) in enumerate(
            (
                (master_keys, master.at[0]),
                (moment_keys, moment.at[0]),
                (master_values, master.at[1]),
                (moment_values, moment.at[1]),
            )
        )
    ]
    blocks = tok.shape[0]
    depth = tok.shape[2]
    if len(tokens.shape) == 3:
        tok_loads = [
            pltpu.make_async_copy(tokens.at[q], tok.at[q], tok_sem.at[q]) for q in range(blocks)
        ]
    else:
        tok_loads = [
            pltpu.make_async_copy(
                tokens.at[:, q * depth : (q + 1) * depth], tok.at[q], tok_sem.at[q]
            )
            for q in range(blocks)
        ]

    def near(s):
        m = jnp.minimum(z, Z - 1 - z)
        half = lax.div(s + 1, 2)
        side = 2 * lax.rem(s + 1, 2) - 1
        beyond = jnp.where(z < Z - 1 - z, s, Z - 1 - s)
        return jnp.where(s <= 2 * m, z + half * side, beyond)

    def far(s):
        return near(Z - 1 - s)

    def steps(count, body, start=0):
        def run(s, carry):
            body(s)
            return carry

        lax.fori_loop(start, count, run, 0)

    def remote(src, dst, send, recv, device):
        return pltpu.make_async_remote_copy(
            src_ref=src,
            dst_ref=dst,
            send_sem=send,
            recv_sem=recv,
            device_id=device,
            device_id_type=MESH,
        )

    def core_copy(kv, p):
        return remote(
            pseudo[kv].at[p, :, oc],
            from_core.at[kv, p],
            rc_s.at[kv, p],
            rc_r.at[kv, p],
            dev(z, y, oc),
        )

    def y_copy(kv, p):
        return remote(
            to_y.at[kv, p], from_y.at[kv, p], ry_s.at[kv, p], ry_r.at[kv, p], dev(z, oy, core)
        )

    def right_copy(kv, p):
        return remote(
            to_z.at[kv, p], from_left.at[kv, p], rz_s.at[kv, p], rl_r.at[kv, p], dev(z + 1, y, core)
        )

    def left_copy(kv, p):
        return remote(
            to_z.at[kv, p], from_right.at[kv, p], rz_s.at[kv, p], rr_r.at[kv, p], dev(z - 1, y, core)
        )

    def w_right(kv, p):
        w = weights.at[kv, p, y, core]
        return remote(w, w, gr_s.at[kv, p], gz_r.at[kv, p], dev(z + 1, y, core))

    def w_left(kv, p):
        w = weights.at[kv, p, y, core]
        return remote(w, w, gl_s.at[kv, p], gz_r.at[kv, p], dev(z - 1, y, core))

    def w_y(kv, p, yy):
        w = weights.at[kv, p, yy, core]
        return remote(w, w, gy_s.at[kv, p], gy_r.at[kv, p], dev(z, oy, core))

    def w_core(kv, p, yy, cc):
        w = weights.at[kv, p, yy, cc]
        return remote(w, w, gc_s.at[kv, p, yy], gc_r.at[kv, p, yy], dev(z, y, oc))

    for copy in loads:
        copy.start()

    barrier = pltpu.get_barrier_semaphore()
    pl.semaphore_signal(barrier, inc=1, device_id=dev(z, y, oc), device_id_type=MESH)
    pl.semaphore_signal(barrier, inc=1, device_id=dev(z, oy, core), device_id_type=MESH)

    @pl.when(z > 0)
    def _():
        pl.semaphore_signal(barrier, inc=1, device_id=dev(z - 1, y, core), device_id_type=MESH)

    @pl.when(z < Z - 1)
    def _():
        pl.semaphore_signal(barrier, inc=1, device_id=dev(z + 1, y, core), device_id_type=MESH)

    peers = 2 + jnp.where(z > 0, 1, 0) + jnp.where(z < Z - 1, 1, 0)
    pl.semaphore_wait(barrier, peers)

    for kv in range(2):
        steps(Z, lambda s: core_copy(kv, far(s)).start())
    for copy in states + tok_loads:
        copy.start()

    for kv in range(2):
        loads[kv].wait()

        def y_send(s):
            p = far(s)
            core_copy(kv, p).wait_recv()
            both = mine[kv, p, oy].astype(F32) + from_core[kv, p, oy].astype(F32)
            to_y[kv, p] = both.astype(BF16)
            y_copy(kv, p).start()

        steps(Z, y_send)

    acc[...] = jnp.zeros_like(acc)

    def reduce_step(kv, s):
        p = far(s)
        y_copy(kv, p).wait_recv()
        total[...] = (
            mine[kv, p, y].astype(F32)
            + from_core[kv, p, y].astype(F32)
            + from_y[kv, p].astype(F32)
        )

        @pl.when((p >= z) & (z > 0))
        def _():
            right_copy(kv, p).wait_recv()
            total[...] += from_left[kv, p].astype(F32)

        @pl.when((p <= z) & (z < Z - 1))
        def _():
            left_copy(kv, p).wait_recv()
            total[...] += from_right[kv, p].astype(F32)

        @pl.when(p != z)
        def _():
            to_z[kv, p] = total[...].astype(BF16)

        @pl.when(p > z)
        def _():
            right_copy(kv, p).start()

        @pl.when(p < z)
        def _():
            left_copy(kv, p).start()

    def nesterov(kv):
        outer_rate = hyper[0]
        outer_mom = hyper[1]
        averaged = total[...] / replicas
        moment_new = outer_mom * moment[kv] + averaged
        master_new = master[kv] - outer_rate * (averaged + outer_mom * moment_new)
        weights[kv, z, y, core] = master_new.astype(BF16)
        master[kv] = master_new
        moment[kv] = moment_new

    def spread(kv, p):
        @pl.when((p <= z) & (z < Z - 1))
        def _():
            w_right(kv, p).start()

        @pl.when((p >= z) & (z > 0))
        def _():
            w_left(kv, p).start()

        w_y(kv, p, y).start()
        w_core(kv, p, y, core).start()

    def gather_step(kv, s):
        p = near(s)
        w_right(kv, p).wait_recv()
        spread(kv, p)

    def dot(kv, p, yy):
        w_core(kv, p, yy, oc).wait_recv()
        q = p * Y + yy
        block = weights[kv, p, yy].reshape(2 * rows, -1)
        tile = min(256, acc.shape[1])

        def one(m, carry):
            span = pl.ds(pl.multiple_of(m * tile, tile), tile)
            acc[kv, span, :] += jnp.dot(tok[q, span, :], block, preferred_element_type=F32)
            return carry

        lax.fori_loop(0, acc.shape[1] // tile, one, 0)

    def y_arrival(kv, s):
        p = near(s)
        w_y(kv, p, oy).wait_recv()
        w_core(kv, p, oy, core).start()

    outs = ((out_master_keys, out_moment_keys), (out_master_values, out_moment_values))

    def stores(kv):
        return [
            pltpu.make_async_copy(master.at[kv], outs[kv][0], store_sem.at[2 * kv]),
            pltpu.make_async_copy(moment.at[kv], outs[kv][1], store_sem.at[2 * kv + 1]),
        ]

    evals = [
        pltpu.make_async_copy(result.at[kv], out, store_sem.at[4 + kv])
        for kv, out in enumerate((eval_keys, eval_values))
    ]

    steps(Z, lambda s: reduce_step(0, s))
    states[0].wait()
    states[1].wait()
    nesterov(0)
    spread(0, z)
    for copy in stores(0):
        copy.start()

    def reduce_and_gather(s):
        reduce_step(1, s)
        gather_step(0, s + 1)

    steps(Z - 1, reduce_and_gather)
    reduce_step(1, Z - 1)
    states[2].wait()
    states[3].wait()
    nesterov(1)
    spread(1, z)
    for copy in stores(1):
        copy.start()
    for copy in tok_loads:
        copy.wait()

    def second(s):
        dot(0, near(s), y)
        gather_step(1, s + 1)
        y_arrival(0, s)

    steps(Z - 1, second)
    y_arrival(0, Z - 1)
    dot(0, near(Z - 1), y)
    steps(Z, lambda s: dot(0, near(s), oy))
    result[0] = acc[0].astype(BF16)
    evals[0].start()
    steps(Z, lambda s: dot(1, near(s), y))

    def last(s):
        y_arrival(1, s)
        dot(1, near(s), oy)

    steps(Z, last)
    result[1] = acc[1].astype(BF16)
    evals[1].start()

    for kv in range(2):

        def drain(p):
            core_copy(kv, p).wait_send()
            y_copy(kv, p).wait_send()

            @pl.when(p != z)
            def _():
                right_copy(kv, p).wait_send()

            @pl.when((p <= z) & (z < Z - 1))
            def _():
                w_right(kv, p).wait_send()

            @pl.when((p >= z) & (z > 0))
            def _():
                w_left(kv, p).wait_send()

            w_y(kv, p, y).wait_send()
            w_core(kv, p, y, core).wait_send()
            w_core(kv, p, oy, core).wait_send()

        steps(Z, drain)
        for copy in stores(kv):
            copy.wait()
    for copy in evals:
        copy.wait()


def body(
    tokens,
    pseudo_keys,
    pseudo_values,
    master_keys,
    moment_keys,
    master_values,
    moment_values,
    outer_hyper,
):
    replicas = lax.axis_size("replica")
    Y = 2
    Z = replicas // (2 * Y)
    width = master_keys.shape[1]
    rows = master_keys.shape[0]
    count = tokens.shape[0]
    blocks = Z * Y
    depth = 2 * rows
    if depth % 128:
        tokens = tokens.reshape(count, blocks, depth).swapaxes(0, 1)
    pseudo_keys, pseudo_values = (
        p.reshape(Z, Y, 2, rows, width) for p in (pseudo_keys, pseudo_values)
    )
    hbm = pl.BlockSpec(memory_space=pl.ANY)
    dma = pltpu.SemaphoreType.DMA
    state = jax.ShapeDtypeStruct(master_keys.shape, F32)
    evaluated = jax.ShapeDtypeStruct((count, width), BF16)
    part = pltpu.VMEM((2, Z, rows, width), BF16)
    pair = pltpu.VMEM((2, Z, Y, rows, width), BF16)
    unit = dma((2, Z))
    return pl.pallas_call(
        functools.partial(kernel, Z, Y, replicas),
        out_shape=(evaluated, evaluated, state, state, state, state),
        in_specs=[hbm] * 7 + [pl.BlockSpec(memory_space=pltpu.SMEM)],
        out_specs=(hbm,) * 6,
        scratch_shapes=[
            pltpu.VMEM((blocks, count, depth), BF16),
            pair,
            pair,
            part,
            part,
            part,
            part,
            part,
            pltpu.VMEM((2, Z, Y, 2, rows, width), BF16),
            pltpu.VMEM((rows, width), F32),
            pltpu.VMEM((2, count, width), F32),
            pltpu.VMEM((2, count, width), BF16),
            pltpu.VMEM((2, rows, width), F32),
            pltpu.VMEM((2, rows, width), F32),
            dma((2,)),
            dma((4,)),
            dma((blocks,)),
            dma((6,)),
            unit,
            unit,
            unit,
            unit,
            unit,
            unit,
            unit,
            unit,
            unit,
            unit,
            unit,
            unit,
            dma((2, Z, Y)),
            dma((2, Z, Y)),
        ],
        compiler_params=pltpu.CompilerParams(
            collective_id=0, has_side_effects=True, vmem_limit_bytes=60 * 1024 * 1024
        ),
        name="outer_step",
    )(
        tokens,
        pseudo_keys,
        pseudo_values,
        master_keys,
        moment_keys,
        master_values,
        moment_values,
        outer_hyper,
    )


def solution(mesh):
    rows = P(("groups", "replica"), None)
    stack = P(("groups", "replica"), None, None)
    return jax.shard_map(
        body,
        mesh=mesh,
        in_specs=(rows, stack, stack, rows, rows, rows, rows, P("groups")),
        out_specs=(rows,) * 6,
        check_vma=False,
    )
```

time: 187 us -> 83.5 us (0.45)
  waiting for transfers between devices: 132 us -> 0 us
  Pallas kernels: 0 us -> 76.5 us
  starting transfers between devices: 18.7 us -> 0 us
  between operations: 14.2 us -> 0.68 us
  matrix products: 10.4 us -> 0 us
  other arithmetic: 6.59 us -> 0 us
    all_to_all x2 -> x0, waiting for transfers between devices: 81.2 us -> none  [the longest x1 40.8 us: body(): lax.all_to_all(blocks_keys, 'replica', split_axis=0, concat_axis=0, tiled...]
    pallas_call x0 -> x1, Pallas kernels: none -> 76.5 us  [body(): pl.pallas_call(functools.partial(kernel, Z, Y, replicas), out_shape=(eval...]
    all_gather x2 -> x0, waiting for transfers between devices: 50.6 us -> none  [the longest x1 36.7 us: body(): lax.all_gather(master_k.astype(jnp.bfloat16), 'replica', axis=0, tiled=True)]
    all_to_all x2 -> x0, starting transfers between devices: 18.6 us -> none  [the longest x1 11.2 us: body(): lax.all_to_all(blocks_keys, 'replica', split_axis=0, concat_axis=0, tiled...]
    dot_general x2 -> x0, matrix products: 10.4 us -> none  [the longest x1 5.2 us: body(): jnp.dot(tokens, whole_values, preferred_element_type=jnp.float32)]
    convert_element_type x2 -> x0, other arithmetic: 4.35 us -> none  [the longest x1 2.2 us: body(): master_v.astype(jnp.bfloat16)]
    reduce_sum x2 -> x0, other arithmetic: 2.24 us -> none  [the longest x1 1.95 us: body(): summed_values = jnp.sum(owned_values.astype(jnp.float32), axis=0)]
    unnamed x14 -> x16, local copies, waits for them, and re-layouts: 4 us -> 6.19 us
  transfers between devices with their start and end apart: 4 -> 0, of which waited for: 4 -> 0; matrix products, arithmetic and copies ran while one was open for 7% -> 0% of each run, Pallas kernels for 0% -> 0%
where the time goes in v1:
time: 83.5 us; the launch traced here: 83.3 us
  Pallas kernels  76.5 us (92%)
  local copies, waits for them, and re-layouts  6.19 us (7%)
    pallas_call x1, Pallas kernels, body(): pl.pallas_call(functools.partial(kernel, Z, Y, replicas), out_shape=(eval...  76.5 us
    unnamed x16, local copies, waits for them, and re-layouts  6.19 us

profile of v1, /device:TPU:0, one launch (start us, length us, event | category | flops | bytes accessed | tf_op | source)
XLA Modules:
  0.0 83.3 jit_solution(10084625207828516358)
XLA Ops:
  0.6 76.5 %outer_step.1 = (bf16[1024,512]{1,0:T(8,128)(2,1)}, bf16[1024,512]{1,0:T(8,128)(2,1)}, f32[128,512]{1,0:T(8,128)}, f32[128,512]{1,0:T(8,128)}, f32[128,512]{1,0:T(8,128)}, /*index=5*/f32[128,512]{1,0:T(8,128)}) custom-call(bf16[1024,2048]{1,0:T(8,128)(2,1)} %tokens.1, bf16[4,2,2,128,512]{4,3,2,1,0:T(8,128)(2,1)} %bitcast.2, ...), custom_call_target="tpu_custom_call" | custom-call | tf_op jit(solution)/shard_map/outer_step/pallas_call | solution.py:405
  77.1 0.0 copy-start
  77.1 0.0 copy-start.4
  77.1 0.0 copy-start.3
  77.1 0.0 copy-start.2
  77.1 2.4 %copy.20 = bf16[1024,512]{1,0:T(8,128)(2,1)} copy(bf16[1024,512]{1,0:T(8,128)(2,1)} %get-tuple-element.12) | data formatting | bytes 2097152
  79.5 0.0 copy-done
  79.5 0.0 copy-start.1
  79.5 1.0 %copy.21 = bf16[1024,512]{1,0:T(8,128)(2,1)} copy(bf16[1024,512]{1,0:T(8,128)(2,1)S(1)} %copy-done) | data formatting | bytes 2097152
  80.5 0.0 copy-done.4
  80.5 0.7 copy.22
  81.2 0.0 copy-done.3
  81.2 0.7 copy.23
  81.9 0.0 copy-done.2
  81.9 0.7 copy.24
  82.6 0.0 copy-done.1
  82.6 0.7 copy.25
Async XLA Ops:
  77.1 2.4 %copy-start = (bf16[1024,512]{1,0:T(8,128)(2,1)S(1)}, bf16[1024,512]{1,0:T(8,128)(2,1)}, u32[]{:S(2)}) copy-start(bf16[1024,512]{1,0:T(8,128)(2,1)} %get-tuple-element.13) | copy-start | bytes 3145732
  77.1 3.4 %copy-start.4 = (f32[128,512]{1,0:T(8,128)S(1)}, f32[128,512]{1,0:T(8,128)}, u32[]{:S(2)}) copy-start(f32[128,512]{1,0:T(8,128)} %get-tuple-element.14) | copy-start | bytes 786436
  77.1 4.1 %copy-start.3 = (f32[128,512]{1,0:T(8,128)S(1)}, f32[128,512]{1,0:T(8,128)}, u32[]{:S(2)}) copy-start(f32[128,512]{1,0:T(8,128)} %get-tuple-element.15) | copy-start | bytes 786436
  77.1 4.8 %copy-start.2 = (f32[128,512]{1,0:T(8,128)S(1)}, f32[128,512]{1,0:T(8,128)}, u32[]{:S(2)}) copy-start(f32[128,512]{1,0:T(8,128)} %get-tuple-element.16) | copy-start | bytes 786436
  79.5 3.1 %copy-start.1 = (f32[128,512]{1,0:T(8,128)S(1)}, f32[128,512]{1,0:T(8,128)}, u32[]{:S(2)}) copy-start(f32[128,512]{1,0:T(8,128)} %get-tuple-element.17) | copy-start | bytes 786436

commit v2 on v1

--- a/solution.py
+++ b/solution.py
@@ -268,18 +268,26 @@
         w_right(kv, p).wait_recv()
         spread(kv, p)
 
-    def dot(kv, p, yy):
-        w_core(kv, p, yy, oc).wait_recv()
-        q = p * Y + yy
-        block = weights[kv, p, yy].reshape(2 * rows, -1)
-        tile = min(256, acc.shape[1])
-
-        def one(m, carry):
+    tile = min(1024, acc.shape[1])
+    cols = 256
+    across = acc.shape[2] // cols
+
+    def dot(kv, p):
+        for yy in range(Y):
+            w_core(kv, p, yy, oc).wait_recv()
+
+        def one(i, carry):
+            m, n = lax.div(i, across), lax.rem(i, across)
             span = pl.ds(pl.multiple_of(m * tile, tile), tile)
-            acc[kv, span, :] += jnp.dot(tok[q, span, :], block, preferred_element_type=F32)
+            lane = pl.ds(pl.multiple_of(n * cols, cols), cols)
+            part = acc[kv, span, lane]
+            for yy in range(Y):
+                block = weights[kv, p, yy, :, :, lane].reshape(2 * rows, cols)
+                part += jnp.dot(tok[p * Y + yy, span, :], block, preferred_element_type=F32)
+            acc[kv, span, lane] = part
             return carry
 
-        lax.fori_loop(0, acc.shape[1] // tile, one, 0)
+        lax.fori_loop(0, acc.shape[1] // tile * across, one, 0)
 
     def y_arrival(kv, s):
         p = near(s)
@@ -307,11 +315,13 @@
     for copy in stores(0):
         copy.start()
 
+    reduce_step(1, 0)
+
     def reduce_and_gather(s):
         reduce_step(1, s)
-        gather_step(0, s + 1)
-
-    steps(Z - 1, reduce_and_gather)
+        gather_step(0, s)
+
+    steps(Z - 1, reduce_and_gather, 1)
     reduce_step(1, Z - 1)
     states[2].wait()
     states[3].wait()
@@ -319,25 +329,23 @@
     spread(1, z)
     for copy in stores(1):
         copy.start()
+    gather_step(0, Z - 1)
     for copy in tok_loads:
         copy.wait()
 
     def second(s):
-        dot(0, near(s), y)
         gather_step(1, s + 1)
         y_arrival(0, s)
 
     steps(Z - 1, second)
     y_arrival(0, Z - 1)
-    dot(0, near(Z - 1), y)
-    steps(Z, lambda s: dot(0, near(s), oy))
+    steps(Z, lambda s: dot(0, near(s)))
     result[0] = acc[0].astype(BF16)
     evals[0].start()
-    steps(Z, lambda s: dot(1, near(s), y))
 
     def last(s):
         y_arrival(1, s)
-        dot(1, near(s), oy)
+        dot(1, near(s))
 
     steps(Z, last)
     result[1] = acc[1].astype(BF16)
@@ -370,6 +378,21 @@
             copy.wait()
     for copy in evals:
         copy.wait()
+
+
+def place(*refs):
+    source, target, held = refs[:6], refs[6:12], refs[12:18]
+    in_sem, out_sem = refs[18:]
+    order = (2, 3, 4, 5, 0, 1)
+    loads = {i: pltpu.make_async_copy(source[i], held[i], in_sem.at[i]) for i in order}
+    stores = {i: pltpu.make_async_copy(held[i], target[i], out_sem.at[i]) for i in order}
+    for i in order:
+        loads[i].start()
+    for i in order:
+        loads[i].wait()
+        stores[i].start()
+    for i in order:
+        stores[i].wait()
 
 
 def body(
@@ -402,7 +425,7 @@
     part = pltpu.VMEM((2, Z, rows, width), BF16)
     pair = pltpu.VMEM((2, Z, Y, rows, width), BF16)
     unit = dma((2, Z))
-    return pl.pallas_call(
+    results = pl.pallas_call(
         functools.partial(kernel, Z, Y, replicas),
         out_shape=(evaluated, evaluated, state, state, state, state),
         in_specs=[hbm] * 7 + [pl.BlockSpec(memory_space=pltpu.SMEM)],
@@ -455,6 +478,14 @@
         moment_values,
         outer_hyper,
     )
+    return pl.pallas_call(
+        place,
+        out_shape=tuple(jax.ShapeDtypeStruct(a.shape, a.dtype) for a in results),
+        in_specs=[hbm] * 6,
+        out_specs=(hbm,) * 6,
+        scratch_shapes=[pltpu.VMEM(a.shape, a.dtype) for a in results] + [dma((6,)), dma((6,))],
+        name="place",
+    )(*results)
 
 
 def solution(mesh):

time: 83.5 us -> 73.9 us (0.89)
  local copies, waits for them, and re-layouts: 6.19 us -> 0 us
  Pallas kernels: 76.5 us -> 73.1 us
    pallas_call x1, Pallas kernels: 76.5 us -> 70.1 us  [body(): pl.pallas_call(functools.partial(kernel, Z, Y, replicas), out_shape=(eval...]
    unnamed x16 -> x0, local copies, waits for them, and re-layouts: 6.19 us -> none
    pallas_call x0 -> x1, Pallas kernels: none -> 2.97 us  [body(): pl.pallas_call(place, out_shape=tuple((jax.ShapeDtypeStruct(a.shape, a.dt...]
where the time goes in v2:
time: 73.9 us; the launch traced here: 73.7 us
  Pallas kernels  73.1 us (99%)
    pallas_call x1, Pallas kernels, body(): pl.pallas_call(functools.partial(kernel, Z, Y, replicas), out_shape=(eval...  70.1 us
    pallas_call x1, Pallas kernels, body(): pl.pallas_call(place, out_shape=tuple((jax.ShapeDtypeStruct(a.shape, a.dt...  2.97 us

profile of v2, /device:TPU:0, one launch (start us, length us, event | category | flops | bytes accessed | tf_op | source)
XLA Modules:
  0.0 73.7 jit_solution(13948613527990069502)
XLA Ops:
  0.6 70.1 %outer_step.1 = (bf16[1024,512]{1,0:T(8,128)(2,1)}, bf16[1024,512]{1,0:T(8,128)(2,1)}, f32[128,512]{1,0:T(8,128)}, f32[128,512]{1,0:T(8,128)}, f32[128,512]{1,0:T(8,128)}, /*index=5*/f32[128,512]{1,0:T(8,128)}) custom-call(bf16[1024,2048]{1,0:T(8,128)(2,1)} %tokens.1, bf16[4,2,2,128,512]{4,3,2,1,0:T(8,128)(2,1)} %bitcast.2, ...), custom_call_target="tpu_custom_call" | custom-call | tf_op jit(solution)/shard_map/outer_step/pallas_call | solution.py:428
  70.8 3.0 %place.1 = (bf16[1024,512]{1,0:T(8,128)(2,1)}, bf16[1024,512]{1,0:T(8,128)(2,1)}, f32[128,512]{1,0:T(8,128)}, f32[128,512]{1,0:T(8,128)}, f32[128,512]{1,0:T(8,128)}, /*index=5*/f32[128,512]{1,0:T(8,128)}) custom-call(bf16[1024,512]{1,0:T(8,128)(2,1)} %get-tuple-element.12.refs_0_, bf16[1024,512]{1,0:T(8,128)(2,1)} %get-tuple-element.13.refs_1_, ...), custom_call_target="tpu_custom_call" | custom-call | tf_op jit(solution)/shard_map/place/pallas_call | solution.py:481
